TPU v7x, 256 devices: a whole 4x4x8 slice. The times are simulated.
256 devices in a mesh: rep: 4 (over x), fsdp: 32 (over y, z), tp: 2 (over core).
Axes of the slice: x: 4, y: 4, z: 8, core: 2. Of those that a mesh axis runs over, the one named last changes fastest.
Arguments:
- saved_inputs: bfloat16 [2, 32768, 768], P(None, ('rep', 'fsdp')), may hold values from -24 to 24
- out_cotangent: float32 [32768, 768], P(('rep', 'fsdp')), may hold values from -1.75 to 1.75
- gate_weight: bfloat16 [2, 768, 4480], P(None, 'fsdp', 'tp'), may hold values from -0.21875 to 0.21875
- up_weight: bfloat16 [2, 768, 4480], P(None, 'fsdp', 'tp'), may hold values from -0.21875 to 0.21875
- down_weight: bfloat16 [2, 768, 4480], P(None, 'fsdp', 'tp'), may hold values from -0.09375 to 0.09375
- norm_gain: bfloat16 [2, 768], P(None, 'fsdp'), may hold values from 0.5 to 1.5
- gate_accum: float32 [2, 768, 4480], P(None, 'fsdp', 'tp'), may hold values from -12 to 12
- up_accum: float32 [2, 768, 4480], P(None, 'fsdp', 'tp'), may hold values from -12 to 12
- down_accum: float32 [2, 768, 4480], P(None, 'fsdp', 'tp'), may hold values from -12 to 12
- gain_accum: float32 [2, 768], P(None, 'fsdp'), may hold values from -12 to 12
Outputs:
- input_cotangent: float32 [32768, 768], P(('rep', 'fsdp'))
- gate_grad: float32 [2, 768, 4480], P(None, 'fsdp', 'tp')
- up_grad: float32 [2, 768, 4480], P(None, 'fsdp', 'tp')
- down_grad: float32 [2, 768, 4480], P(None, 'fsdp', 'tp')
- gain_grad: float32 [2, 768], P(None, 'fsdp')
All inputs are finite; a program needn't handle non-finite values.
Results may differ from a plain program's by a relative error of at most 0.0025.
Values may be sent and summed in bfloat16 or wider, within the bound.
No kernel may reach another device: no remote copies, remote signals or barrier semaphores. Data moves between devices by JAX's collectives and lax.ppermute only.
A program may use at most 192 MiB of HBM per device.

v0:
```python
import jax
import jax.numpy as jnp
from jax import lax
from jax.sharding import PartitionSpec as P

epsilon = 1e-06


def as_sent(value):

    def short(part):
        return part.astype(jnp.bfloat16) if part.dtype == jnp.float32 else part

    return jax.tree.map(short, value)


def total_of_pieces(value, axis):
    return lax.all_gather(value, axis).sum(0)


def scattered(product, width, axis):
    everything = product(jnp.int32(0), lax.axis_size(axis) * width)
    own = lax.psum_scatter(everything, axis, scatter_dimension=0, tiled=True)
    return own


def fetch_layer(weight_stacks, layer_index):
    pieces = tuple(
        (
            lax.dynamic_index_in_dim(weight_stack, layer_index, 0, keepdims=False)
            for weight_stack in weight_stacks
        )
    )
    return (
        lax.all_gather(as_sent(pieces[0]), "fsdp", axis=0, tiled=True),
        lax.all_gather(as_sent(pieces[1]), "fsdp", axis=0, tiled=True),
        lax.all_gather(as_sent(pieces[2]), "fsdp", axis=0, tiled=True),
        lax.all_gather(as_sent(pieces[3]), "fsdp", axis=0, tiled=True),
    )


def layer_backward(saved_x, cotangent, weights):
    gate_full, up_full, down_full, gain_full = weights
    feature_count = saved_x.shape[1]
    inputs = saved_x.astype(jnp.float32)
    tok_scale = lax.rsqrt(jnp.mean(inputs * inputs, axis=1, keepdims=True) + epsilon)
    whitened = inputs * tok_scale
    gain_vec = gain_full.astype(jnp.float32)
    normed = (whitened * gain_vec).astype(jnp.bfloat16)
    gate_pre = jnp.dot(normed, gate_full, preferred_element_type=jnp.float32)
    up_pre = jnp.dot(normed, up_full, preferred_element_type=jnp.float32)
    sigmoid_gate = jax.nn.sigmoid(gate_pre)
    active = gate_pre * sigmoid_gate
    hidden = (active * up_pre).astype(jnp.bfloat16)
    upstream = cotangent.astype(jnp.bfloat16)
    grad_hidden = jnp.dot(upstream, down_full, preferred_element_type=jnp.float32)
    grad_gate = (
        grad_hidden * up_pre * (sigmoid_gate * (1.0 + gate_pre * (1.0 - sigmoid_gate)))
    ).astype(jnp.bfloat16)
    grad_up = (grad_hidden * active).astype(jnp.bfloat16)
    contract_cols = (((1,), (1,)), ((), ()))
    partial_grad = lax.dot_general(
        grad_gate, gate_full, contract_cols, preferred_element_type=jnp.float32
    )
    partial_grad = partial_grad + lax.dot_general(
        grad_up, up_full, contract_cols, preferred_element_type=jnp.float32
    )
    grad_normed = total_of_pieces(partial_grad, "tp")
    grad_white = grad_normed * gain_vec
    inner_mean = jnp.mean(grad_white * whitened, axis=1, keepdims=True)
    passed = cotangent + tok_scale * (grad_white - whitened * inner_mean)
    gain_total = jnp.sum(grad_normed * whitened, axis=0)
    contract_rows = (((0,), (0,)), ((), ()))

    def grad_term(row_start, row_count):
        rows_normed = lax.dynamic_slice_in_dim(normed, row_start, row_count, 1)
        rows_upstream = lax.dynamic_slice_in_dim(upstream, row_start, row_count, 1)
        gate_part = lax.dot_general(
            rows_normed, grad_gate, contract_rows, preferred_element_type=jnp.float32
        )
        up_part = lax.dot_general(
            rows_normed, grad_up, contract_rows, preferred_element_type=jnp.float32
        )
        down_part = lax.dot_general(
            rows_upstream, hidden, contract_rows, preferred_element_type=jnp.float32
        )
        gain_part = lax.dynamic_slice_in_dim(gain_total, row_start, row_count, 0)[:, None]
        return jnp.concatenate([gate_part, up_part, down_part, gain_part], axis=1)

    grad_shard = scattered(grad_term, feature_count // lax.axis_size("fsdp"), "fsdp")
    grad_shard = grad_shard
    return (passed, grad_shard)


def body(
    saved_inputs,
    out_cotangent,
    gate_weight,
    up_weight,
    down_weight,
    norm_gain,
    gate_accum,
    up_accum,
    down_accum,
    gain_accum,
):
    layers = saved_inputs.shape[0]
    hidden_local = gate_weight.shape[2]
    weight_stacks = (gate_weight, up_weight, down_weight, norm_gain)

    def layer_step(carry, slices):
        cotangent, weights = carry
        saved_x, layer_index = slices
        upcoming = fetch_layer(weight_stacks, layer_index - 1)
        passed, grad_shard = layer_backward(saved_x, cotangent, weights)
        return ((passed, upcoming), grad_shard)

    current = fetch_layer(weight_stacks, layers - 1)
    indices = jnp.arange(1, layers, dtype=jnp.int32)
    (passed, lowest), upper_shards = lax.scan(
        layer_step, (out_cotangent, current), (saved_inputs[1:], indices), reverse=True
    )
    cotangent, first_shard = layer_backward(saved_inputs[0], passed, lowest)
    shards = jnp.concatenate([first_shard[None], upper_shards], axis=0)
    shards = lax.psum(shards, "rep")
    gate_grad = gate_accum + shards[:, :, :hidden_local]
    up_grad = up_accum + shards[:, :, hidden_local : 2 * hidden_local]
    down_grad = down_accum + shards[:, :, 2 * hidden_local : 3 * hidden_local]
    gain_grad = gain_accum + shards[:, :, 3 * hidden_local]
    return (cotangent, gate_grad, up_grad, down_grad, gain_grad)


def solution(mesh):
    return jax.shard_map(
        body,
        mesh=mesh,
        in_specs=(
            P(None, ("rep", "fsdp"), None),
            P(("rep", "fsdp"), None),
            P(None, "fsdp", "tp"),
            P(None, "fsdp", "tp"),
            P(None, "fsdp", "tp"),
            P(None, "fsdp"),
            P(None, "fsdp", "tp"),
            P(None, "fsdp", "tp"),
            P(None, "fsdp", "tp"),
            P(None, "fsdp"),
        ),
        out_specs=(
            P(("rep", "fsdp"), None),
            P(None, "fsdp", "tp"),
            P(None, "fsdp", "tp"),
            P(None, "fsdp", "tp"),
            P(None, "fsdp"),
        ),
        check_vma=False,
    )
```

profile of v0, /device:TPU:8, one launch (start us, length us, event | category | flops | bytes accessed | tf_op | source)
XLA Modules:
  0.0 1303.9 jit_solution(17717513750796125036)
XLA Ops:
  7.2 0.0 all-gather.21.cloned.1.call-start
  7.2 1.7 fusion.71
  9.0 0.0 all-gather.23.cloned.1.call-start
  9.0 1.6 fusion.73
  10.7 0.0 all-gather.19.cloned.1.call-start
  10.7 1.7 fusion.72
  12.4 0.0 all-gather.25.cloned.1.call-start
  12.5 1.4 fusion.74
  14.5 0.7 slice_bitcast_fusion
  15.2 0.2 dynamic-update-slice
  15.4 0.2 dynamic-update-slice.1
  15.6 66.2 %all-reduce.5 = (bf16[768]{0:T(1024)(128)(2,1)S(1)}, bf16[768]{0:T(1024)(128)(2,1)S(1)}) all-reduce(bf16[768]{0:T(1024)(128)(2,1)S(1)} %dynamic-update-slice, bf16[768]{0:T(1024)(128)(2,1)S(1)} %dynamic-update-slice.1), channel_id=3, replica_groups=mesh['rep'=4,'fsdp'=32,'tp'=2] {'fsdp'}, use_global_device_ids=true, to_apply=%add | all-reduce | flops 1536 | bytes 6144
  81.9 1.2 fusion.43
  83.0 10.2 all-gather.21.cloned.1.call-done
  93.2 3.5 fusion.16
  96.8 76.8 %all-gather.23.cloned.1.call-done = bf16[1,768,2240]{2,1,0:T(8,128)(2,1)} async-done(((bf16[1,24,2240]{2,1,0:T(8,128)(2,1)}), bf16[1,768,2240]{2,1,0:T(8,128)(2,1)}) %all-gather.23.cloned.1.call-update) | async-done | bytes 3440656 | tf_op jit(solution)/shard_map/all_gather | solution.py:35
  173.5 5.0 fusion.12
  178.5 74.8 %all-gather.19.cloned.1.call-done = bf16[1,768,2240]{2,1,0:T(8,128)(2,1)} async-done(((bf16[1,24,2240]{2,1,0:T(8,128)(2,1)}), bf16[1,768,2240]{2,1,0:T(8,128)(2,1)}) %all-gather.19.cloned.1.call-update) | async-done | bytes 3440656 | tf_op jit(solution)/shard_map/all_gather | solution.py:37
  253.3 5.2 multiply_convert_fusion.4
  258.5 1.1 fusion.10
  259.6 0.2 copy-done.8
  259.8 1.5 copy-done.1
  261.3 2.1 fusion.22
  263.4 0.0 all-gather.31.cloned.1.call-start
  263.4 0.5 all-gather.31.cloned.1.call-update
  264.0 0.5 all-gather.29.cloned.1.call-update
  264.6 0.7 all-gather.27.cloned.1.call-update
  265.3 0.2 all-gather.33.cloned.1.call-start
  265.6 5.4 fusion.65
  271.0 4.1 fusion.67
  275.1 4.1 convolution_bitcast_fusion
  279.2 1.7 reduce_sum.77
  280.8 0.4 fusion.42
  281.3 0.2 fusion.41
  281.6 78.6 %all-gather.31.cloned.1.call-done = bf16[1,768,2240]{2,1,0:T(8,128)(2,1)} async-done(((bf16[1,24,2240]{2,1,0:T(8,128)(2,1)}), bf16[1,768,2240]{2,1,0:T(8,128)(2,1)}) %all-gather.31.cloned.1.call-update) | async-done | bytes 3440656 | tf_op jit(solution)/shard_map/while/body/eval_jaxpr/all_gather | solution.py:35
  360.1 5.0 fusion.2
  365.1 75.2 %all-gather.29.cloned.1.call-done = bf16[1,768,2240]{2,1,0:T(8,128)(2,1)} async-done(((bf16[1,24,2240]{2,1,0:T(8,128)(2,1)}), bf16[1,768,2240]{2,1,0:T(8,128)(2,1)}) %all-gather.29.cloned.1.call-update) | async-done | bytes 3440656 | tf_op jit(solution)/shard_map/while/body/eval_jaxpr/all_gather | solution.py:36
  440.3 3.7 fusion.6
  444.0 1.3 copy-done.7
  445.4 4.2 fusion.28
  449.6 70.4 %all-gather.27.cloned.1.call-done = bf16[1,768,2240]{2,1,0:T(8,128)(2,1)} async-done(((bf16[1,24,2240]{2,1,0:T(8,128)(2,1)}), bf16[1,768,2240]{2,1,0:T(8,128)(2,1)}) %all-gather.27.cloned.1.call-update) | async-done | bytes 3440656 | tf_op jit(solution)/shard_map/while/body/eval_jaxpr/all_gather | solution.py:37
  520.1 5.4 multiply_convert_fusion.2
  525.5 4.3 fusion.59
  529.8 1.2 fusion
  531.0 0.8 copy-done.4
  531.8 2.1 fusion.25
  533.9 0.0 all-reduce.11.cloned.1.call-start
  533.9 3.9 fusion.61
  537.8 15.0 %pad_maximum_fusion.1 = f32[768,6721]{0,1:T(8,128)} fusion(f32[768,1]{0,1:T(1,128)S(1)} %broadcast_in_dim.29, f32[768,2240]{0,1:T(8,128)} %convolution_bitcast_fusion, f32[768,2240]{0,1:T(8,128)} %fusion.67, f32[768,2240]{0,1:T(8,128)} %fusion.65), kind=kLoop, calls=%fused_computation.1 | loop fusion | flops 15485184 | bytes 41293824 | tf_op jit(solution)/shard_map/while/body/eval_jaxpr/concatenate | solution.py:88
  552.9 1.6 reduce_sum.80
  554.5 0.4 fusion.49
  554.8 15.0 %pad_maximum_fusion = f32[768,6721]{0,1:T(8,128)} fusion(f32[768,1]{0,1:T(1,128)S(1)} %broadcast_in_dim.27, f32[768,2240]{0,1:T(8,128)} %fusion.28, f32[768,2240]{0,1:T(8,128)} %fusion.61, f32[768,2240]{0,1:T(8,128)} %fusion.59), kind=kLoop, calls=%fused_computation | loop fusion | flops 15485184 | bytes 41293824 | tf_op jit(solution)/shard_map/concatenate | solution.py:88
  569.8 0.0 all-reduce.9.cloned.1.call-start
  570.5 650.6 %all-reduce.11.cloned.1.call-done = (f32[768,6721]{0,1:T(8,128)}, f32[768,6721]{0,1:T(8,128)}) async-done(((f32[768,6721]{0,1:T(8,128)}, f32[768,6721]{0,1:T(8,128)}), (f32[768,6721]{0,1:T(8,128)}, f32[768,6721]{0,1:T(8,128)})) %all-reduce.11.cloned.1.call-update) | async-done | bytes 41293840
  1221.2 5.7 dynamic-slice_bitcast_fusion
  1226.8 5.8 dynamic-slice_bitcast_fusion.1
  1232.7 2.6 copy.23
  1235.3 3.2 copy.24
  1238.6 2.2 pad_maximum_fusion.2
  1240.8 1.1 fusion.48
  1242.0 51.0 %all-reduce.9.cloned.1.call-done = f32[2,24,6721]{2,1,0:T(8,128)} async-done(((f32[2,24,6721]{2,1,0:T(8,128)}), f32[2,24,6721]{2,1,0:T(8,128)}) %all-reduce.9.cloned.1.call-update) | async-done | bytes 1290448 | tf_op jit(solution)/shard_map/psum | solution.py:125
  1292.9 0.9 slice_reduce_fusion
  1293.8 0.6 add.92
  1294.4 2.7 slice_add_fusion
  (48 shorter events, 0.3 us)
Async XLA Ops:
  7.2 86.1 %copy-start = (bf16[2,256,768]{2,1,0:T(8,128)(2,1)S(1)}, bf16[2,256,768]{2,1,0:T(8,128)(2,1)}, u32[]{:S(2)}) copy-start(bf16[2,256,768]{2,1,0:T(8,128)(2,1)} %param.10) | copy-start | bytes 2359300
  7.2 86.0 %all-gather.21.cloned.1.call-start = ((), (), s32[]{:S(2)}) async-start(), calls=%async_computation.2 | async-start | bytes 3649536 | tf_op jit(solution)/shard_map/all_gather | solution.py:36
  9.0 164.6 %all-gather.23.cloned.1.call-start = ((), (), s32[]{:S(2)}) async-start(), calls=%async_computation.3 | async-start | bytes 3649536 | tf_op jit(solution)/shard_map/all_gather | solution.py:35
  10.7 242.6 %all-gather.19.cloned.1.call-start = ((), (), s32[]{:S(2)}) async-start(), calls=%async_computation.1 | async-start | bytes 3649536 | tf_op jit(solution)/shard_map/all_gather | solution.py:37
  12.4 266.8 %all-gather.25.cloned.1.call-start = ((), (), s32[]{:S(2)}) async-start(), calls=%async_computation.4 | async-start | bytes 2359296 | tf_op jit(solution)/shard_map/while/body/eval_jaxpr/all_gather | solution.py:18
  253.3 5.2 copy-start.2
  258.4 1.2 copy-start.10
  258.5 1.4 copy-start.8
  258.5 2.8 copy-start.1
  263.4 96.8 %all-gather.31.cloned.1.call-start = ((), (), s32[]{:S(2)}) async-start(), calls=%async_computation.7 | async-start | bytes 3649536 | tf_op jit(solution)/shard_map/while/body/eval_jaxpr/all_gather | solution.py:35
  264.0 176.3 %all-gather.29.cloned.1.call-start = ((), (), s32[]{:S(2)}) async-start(), calls=%async_computation.6 | async-start | bytes 3649536 | tf_op jit(solution)/shard_map/while/body/eval_jaxpr/all_gather | solution.py:36
  264.6 255.5 %all-gather.27.cloned.1.call-start = ((), (), s32[]{:S(2)}) async-start(), calls=%async_computation.5 | async-start | bytes 3649536 | tf_op jit(solution)/shard_map/while/body/eval_jaxpr/all_gather | solution.py:37
  265.3 287.6 %all-gather.33.cloned.1.call-start = ((), (), s32[]{:S(2)}) async-start(), calls=%async_computation.8 | async-start | bytes 2359296 | tf_op jit(solution)/shard_map/all_gather | solution.py:18
  265.5 5.4 copy-start.9
  270.9 4.1 copy-start.5
  270.9 4.1 copy-start.11
  279.2 2.1 copy-start.12
  440.3 5.1 copy-start.6
  444.0 1.4 copy-start.7
  525.5 4.3 copy-start.3
  529.8 2.0 copy-start.4
  533.9 687.3 %all-reduce.11.cloned.1.call-start = ((), (), s32[]{:S(2)}) async-start(), calls=%async_computation.9 | async-start | bytes 82673664
  569.8 723.1 %all-reduce.9.cloned.1.call-start = ((), (), s32[]{:S(2)}) async-start(), calls=%async_computation | async-start | bytes 2605056 | tf_op jit(solution)/shard_map/psum | solution.py:125
  1240.8 53.0 %copy-start.15 = (f32[2,24]{1,0:T(2,128)S(1)}, f32[2,24]{1,0:T(2,128)}, u32[]{:S(2)}) copy-start(f32[2,24]{1,0:T(2,128)} %param.19) | copy-start | bytes 580
  1240.8 53.6 %copy-start.13 = (f32[2,24,2240]{2,1,0:T(8,128)S(1)}, f32[2,24,2240]{2,1,0:T(8,128)}, u32[]{:S(2)}) copy-start(f32[2,24,2240]{2,1,0:T(8,128)} %param.18) | copy-start | bytes 1290244
  1240.8 53.6 %copy-start.14 = (f32[2,24,2240]{2,1,0:T(8,128)S(1)}, f32[2,24,2240]{2,1,0:T(8,128)}, u32[]{:S(2)}) copy-start(f32[2,24,2240]{2,1,0:T(8,128)} %param.17) | copy-start | bytes 1290244
Sparse Core Ops, SparseCore 0:
  11.2 82.0 all-gather.20
  96.4 77.0 all-gather.22
  176.1 77.1 all-gather.18
  263.5 13.1 all-gather.24
  279.7 80.3 all-gather.30
  363.2 77.1 all-gather.28
  442.9 77.1 all-gather.26
  534.0 13.1 all-gather.32
  569.9 651.1 all-reduce.10
  1241.0 51.9 all-reduce.8
where the time goes:
time: 1300 us
  waiting for transfers between devices  1090 us (84%)
  blocking collectives  66.2 us (5%)
  matrix products  60.3 us (5%)
  other arithmetic  42 us (3%)
  local copies, waits for them, and re-layouts  29.7 us (2%)
  between operations  15.7 us (1%)
    unnamed x11, waiting for transfers between devices  653 us
    all_gather x2, waiting for transfers between devices, fetch_layer(): lax.all_gather(as_sent(pieces[0]), 'fsdp', axis=0, tiled=True)  155 us
    all_gather x2, waiting for transfers between devices, fetch_layer(): lax.all_gather(as_sent(pieces[2]), 'fsdp', axis=0, tiled=True)  145 us
    all_gather x2, waiting for transfers between devices, fetch_layer(): lax.all_gather(as_sent(pieces[1]), 'fsdp', axis=0, tiled=True)  85.4 us
    unnamed x1, blocking collectives  66.2 us
    psum x1, waiting for transfers between devices, body(): shards = lax.psum(shards, 'rep')  51 us
    concatenate x2, other arithmetic, grad_term(): return jnp.concatenate([gate_part, up_part, down_part, gain_part], axis=1)  30 us
  transfers between devices with their start and end apart: 10, of which 8 were waited for; matrix products, arithmetic and copies ran while one was open for 5% of the time, Pallas kernels for 0%

commit v1 on v0

--- a/solution.py
+++ b/solution.py
@@ -4,6 +4,11 @@
 from jax.sharding import PartitionSpec as P
 
 epsilon = 1e-06
+
+
+def tiled_gather(shard, axis, dim):
+    copies = jnp.concatenate([shard] * lax.axis_size(axis), axis=dim)
+    return lax.all_to_all(copies, axis, dim, dim, tiled=True)
 
 
 def as_sent(value):
@@ -34,7 +39,7 @@
     return (
         lax.all_gather(as_sent(pieces[0]), "fsdp", axis=0, tiled=True),
         lax.all_gather(as_sent(pieces[1]), "fsdp", axis=0, tiled=True),
-        lax.all_gather(as_sent(pieces[2]), "fsdp", axis=0, tiled=True),
+        tiled_gather(as_sent(pieces[2]), "fsdp", 0),
         lax.all_gather(as_sent(pieces[3]), "fsdp", axis=0, tiled=True),
     )
 

time: 1300 us -> 1210 us (0.931)
  waiting for transfers between devices: 1090 us -> 889 us
  blocking collectives: 66.2 us -> 151 us
  starting transfers between devices: 0.58 us -> 19.3 us
    all_gather x2 -> x0, waiting for transfers between devices: 145 us -> none  [fetch_layer(): lax.all_gather(as_sent(pieces[2]), 'fsdp', axis=0, tiled=True)]
    unnamed x1, blocking collectives: 66.2 us -> 151 us
    all_gather x2, waiting for transfers between devices: 155 us -> 109 us  [fetch_layer(): lax.all_gather(as_sent(pieces[0]), 'fsdp', axis=0, tiled=True)]
    all_to_all x0 -> x2, starting transfers between devices: none -> 18.8 us  [tiled_gather(): return lax.all_to_all(copies, axis, dim, dim, tiled=True)]
    unnamed x11 -> x9, waiting for transfers between devices: 653 us -> 652 us
  transfers between devices with their start and end apart: 10 -> 10, of which waited for: 8 -> 5; matrix products, arithmetic and copies ran while one was open for 5% -> 6% of each run, Pallas kernels for 0% -> 0%
where the time goes in v1:
time: 1210 us
  waiting for transfers between devices  889 us (73%)
  blocking collectives  151 us (12%)
  matrix products  61.1 us (5%)
  other arithmetic  41.5 us (3%)
  local copies, waits for them, and re-layouts  36.2 us (3%)
  starting transfers between devices  19.3 us (2%)
  between operations  16 us (1%)
    unnamed x9, waiting for transfers between devices  652 us
    unnamed x1, blocking collectives  151 us
    all_gather x2, waiting for transfers between devices, fetch_layer(): lax.all_gather(as_sent(pieces[0]), 'fsdp', axis=0, tiled=True)  109 us
    all_gather x2, waiting for transfers between devices, fetch_layer(): lax.all_gather(as_sent(pieces[1]), 'fsdp', axis=0, tiled=True)  76.2 us
    psum x1, waiting for transfers between devices, body(): shards = lax.psum(shards, 'rep')  51.2 us
    concatenate x2, other arithmetic, grad_term(): return jnp.concatenate([gate_part, up_part, down_part, gain_part], axis=1)  30.2 us
  transfers between devices with their start and end apart: 10, of which 5 were waited for; matrix products, arithmetic and copies ran while one was open for 6% of the time, Pallas kernels for 0%

profile of v1, /device:TPU:8, one launch (start us, length us, event | category | flops | bytes accessed | tf_op | source)
XLA Modules:
  0.0 1213.3 jit_solution(959273399058549291)
XLA Ops:
  7.2 1.7 fusion.68
  9.0 1.6 fusion.69
  10.7 0.9 constant_dynamic-update-slice_fusion.63
  11.6 1.0 constant_dynamic-update-slice_fusion.62
  12.5 1.0 constant_dynamic-update-slice_fusion.61
  13.5 1.0 constant_dynamic-update-slice_fusion.60
  14.5 1.0 constant_dynamic-update-slice_fusion.59
  15.5 1.0 constant_dynamic-update-slice_fusion.58
  17.1 1.7 copy-done.3
  18.9 1.8 copy-done.2
  20.6 11.9 all-to-all-start
  32.5 0.0 all-gather.19.cloned.1.call-start
  32.6 0.7 fusion.70
  34.0 0.2 dynamic-update-slice
  34.2 0.2 dynamic-update-slice.1
  34.4 150.6 %all-reduce.5 = (bf16[768]{0:T(1024)(128)(2,1)S(1)}, bf16[768]{0:T(1024)(128)(2,1)S(1)}) all-reduce(bf16[768]{0:T(1024)(128)(2,1)S(1)} %dynamic-update-slice, bf16[768]{0:T(1024)(128)(2,1)S(1)} %dynamic-update-slice.1), channel_id=2, replica_groups=mesh['rep'=4,'fsdp'=32,'tp'=2] {'fsdp'}, use_global_device_ids=true, to_apply=%add | all-reduce | flops 1536 | bytes 6144
  185.0 0.2 fusion.39
  185.2 3.6 fusion.14
  188.8 24.1 %all-gather.17.cloned.1.call-done = bf16[1,768,2240]{2,1,0:T(8,128)(2,1)} async-done(((bf16[1,24,2240]{2,1,0:T(8,128)(2,1)}), bf16[1,768,2240]{2,1,0:T(8,128)(2,1)}) %all-gather.17.cloned.1.call-update) | async-done | bytes 3440656 | tf_op jit(solution)/shard_map/all_gather | solution.py:40
  212.9 4.9 fusion.10
  217.8 4.9 multiply_convert_fusion.4
  222.8 1.1 fusion.8
  224.0 0.3 copy-done.11
  224.2 1.4 copy-done.4
  225.6 2.0 fusion.18
  227.7 0.5 all-gather.23.cloned.1.call-update
  228.3 0.5 all-gather.21.cloned.1.call-update
  228.8 7.0 all-to-all-start.1
  235.8 0.2 all-gather.25.cloned.1.call-start
  236.1 5.5 fusion.62
  241.5 3.9 fusion.64
  245.4 4.2 convolution_bitcast_fusion
  249.6 1.7 reduce_sum.77
  251.3 0.4 fusion.38
  251.8 0.2 fusion.37
  252.0 85.2 %all-gather.23.cloned.1.call-done = bf16[1,768,2240]{2,1,0:T(8,128)(2,1)} async-done(((bf16[1,24,2240]{2,1,0:T(8,128)(2,1)}), bf16[1,768,2240]{2,1,0:T(8,128)(2,1)}) %all-gather.23.cloned.1.call-update) | async-done | bytes 3440656 | tf_op jit(solution)/shard_map/while/body/eval_jaxpr/all_gather | solution.py:40
  337.3 4.9 fusion.2
  342.2 76.2 %all-gather.21.cloned.1.call-done = bf16[1,768,2240]{2,1,0:T(8,128)(2,1)} async-done(((bf16[1,24,2240]{2,1,0:T(8,128)(2,1)}), bf16[1,768,2240]{2,1,0:T(8,128)(2,1)}) %all-gather.21.cloned.1.call-update) | async-done | bytes 3440656 | tf_op jit(solution)/shard_map/while/body/eval_jaxpr/all_gather | solution.py:41
  418.3 3.7 fusion.6
  422.1 1.4 copy-done.10
  423.5 4.2 fusion.24
  427.7 5.5 multiply_convert_fusion.2
  433.2 4.2 fusion.56
  437.4 1.2 fusion
  438.6 0.8 copy-done.7
  439.4 2.1 fusion.21
  441.5 0.0 all-reduce.11.cloned.1.call-start
  441.6 5.2 fusion.58
  446.8 15.1 %pad_maximum_fusion.1 = f32[768,6721]{0,1:T(8,128)} fusion(f32[768,1]{0,1:T(1,128)S(1)} %broadcast_in_dim.29, f32[768,2240]{0,1:T(8,128)} %convolution_bitcast_fusion, f32[768,2240]{0,1:T(8,128)} %fusion.64, f32[768,2240]{0,1:T(8,128)} %fusion.62), kind=kLoop, calls=%fused_computation.1 | loop fusion | flops 15485184 | bytes 41293824 | tf_op jit(solution)/shard_map/while/body/eval_jaxpr/concatenate | solution.py:93
  461.9 1.6 reduce_sum.80
  463.5 0.4 fusion.45
  463.9 15.1 %pad_maximum_fusion = f32[768,6721]{0,1:T(8,128)} fusion(f32[768,1]{0,1:T(1,128)S(1)} %broadcast_in_dim.27, f32[768,2240]{0,1:T(8,128)} %fusion.24, f32[768,2240]{0,1:T(8,128)} %fusion.58, f32[768,2240]{0,1:T(8,128)} %fusion.56), kind=kLoop, calls=%fused_computation | loop fusion | flops 15485184 | bytes 41293824 | tf_op jit(solution)/shard_map/concatenate | solution.py:93
  479.1 0.0 all-reduce.9.cloned.1.call-start
  479.8 650.7 %all-reduce.11.cloned.1.call-done = (f32[768,6721]{0,1:T(8,128)}, f32[768,6721]{0,1:T(8,128)}) async-done(((f32[768,6721]{0,1:T(8,128)}, f32[768,6721]{0,1:T(8,128)}), (f32[768,6721]{0,1:T(8,128)}, f32[768,6721]{0,1:T(8,128)})) %all-reduce.11.cloned.1.call-update) | async-done | bytes 41293840
  1130.4 5.6 dynamic-slice_bitcast_fusion
  1136.1 5.7 dynamic-slice_bitcast_fusion.1
  1141.7 2.6 copy.23
  1144.4 3.2 copy.24
  1147.6 2.3 pad_maximum_fusion.2
  1150.0 1.1 fusion.44
  1151.1 51.2 %all-reduce.9.cloned.1.call-done = f32[2,24,6721]{2,1,0:T(8,128)} async-done(((f32[2,24,6721]{2,1,0:T(8,128)}), f32[2,24,6721]{2,1,0:T(8,128)}) %all-reduce.9.cloned.1.call-update) | async-done | bytes 1290448 | tf_op jit(solution)/shard_map/psum | solution.py:130
  1202.3 0.9 slice_reduce_fusion
  1203.2 0.6 add.92
  1203.8 2.7 slice_add_fusion
  (90 shorter events, 0.9 us)
Async XLA Ops:
  7.2 9.3 copy-start
  7.2 178.0 %all-gather.15.cloned.1.call-start = ((), (), s32[]{:S(2)}) async-start(), calls=%async_computation.3 | async-start | bytes 3649536 | tf_op jit(solution)/shard_map/all_gather | solution.py:41
  8.9 204.0 %all-gather.17.cloned.1.call-start = ((), (), s32[]{:S(2)}) async-start(), calls=%async_computation.4 | async-start | bytes 3649536 | tf_op jit(solution)/shard_map/all_gather | solution.py:40
  17.1 1.8 copy-start.3
  18.9 1.8 copy-start.2
  20.6 12.0 copy-start.21
  20.6 13.3 %copy-start.19 = (bf16[2,24]{1,0:T(2,128)(2,1)S(1)}, bf16[2,24]{1,0:T(2,128)(2,1)}, u32[]{:S(2)}) copy-start(bf16[2,24]{1,0:T(2,128)(2,1)} %param.15) | copy-start | bytes 292
  20.6 164.3 %copy-start.1 = (bf16[2,256,768]{2,1,0:T(8,128)(2,1)S(1)}, bf16[2,256,768]{2,1,0:T(8,128)(2,1)}, u32[]{:S(2)}) copy-start(bf16[2,256,768]{2,1,0:T(8,128)(2,1)} %param.10) | copy-start | bytes 2359300
  20.6 197.2 %all-to-all-start = ((bf16[32,24,2240]{2,1,0:T(8,128)(2,1)}), bf16[32,24,2240]{2,1,0:T(8,128)(2,1)}, u32[]{:S(2)}, u32[]{:S(2)}) async-start(bf16[32,24,2240]{2,1,0:T(8,128)(2,1)} %bitcast.146), calls=%async_computation | async-start | bytes 7077888 | tf_op jit(solution)/shard_map/all_to_all | solution.py:11
  32.5 217.1 %all-gather.19.cloned.1.call-start = ((), (), s32[]{:S(2)}) async-start(), calls=%async_computation.5 | async-start | bytes 2359296 | tf_op jit(solution)/shard_map/while/body/eval_jaxpr/all_gather | solution.py:23
  217.8 5.0 copy-start.5
  222.8 1.2 copy-start.13
  222.8 1.5 copy-start.11
  222.8 2.8 copy-start.4
  227.7 109.6 %all-gather.23.cloned.1.call-start = ((), (), s32[]{:S(2)}) async-start(), calls=%async_computation.7 | async-start | bytes 3649536 | tf_op jit(solution)/shard_map/while/body/eval_jaxpr/all_gather | solution.py:40
  228.2 190.1 %all-gather.21.cloned.1.call-start = ((), (), s32[]{:S(2)}) async-start(), calls=%async_computation.6 | async-start | bytes 3649536 | tf_op jit(solution)/shard_map/while/body/eval_jaxpr/all_gather | solution.py:41
  228.8 198.9 %all-to-all-start.1 = ((bf16[32,24,2240]{2,1,0:T(8,128)(2,1)}), bf16[32,24,2240]{2,1,0:T(8,128)(2,1)}, u32[]{:S(2)}, u32[]{:S(2)}) async-start(bf16[32,24,2240]{2,1,0:T(8,128)(2,1)} %bitcast.147), calls=%async_computation.1 | async-start | bytes 7077888 | tf_op jit(solution)/shard_map/while/body/eval_jaxpr/all_to_all | solution.py:11
  235.8 226.1 %all-gather.25.cloned.1.call-start = ((), (), s32[]{:S(2)}) async-start(), calls=%async_computation.8 | async-start | bytes 2359296 | tf_op jit(solution)/shard_map/all_gather | solution.py:23
  236.0 5.5 copy-start.12
  241.5 3.9 copy-start.8
  241.5 3.9 copy-start.15
  249.6 2.2 copy-start.16
  418.3 5.1 copy-start.9
  422.1 1.4 copy-start.10
  433.2 5.4 copy-start.14
  433.2 4.2 copy-start.6
  437.4 2.0 copy-start.7
  441.5 688.9 %all-reduce.11.cloned.1.call-start = ((), (), s32[]{:S(2)}) async-start(), calls=%async_computation.9 | async-start | bytes 82673664
  479.1 723.3 %all-reduce.9.cloned.1.call-start = ((), (), s32[]{:S(2)}) async-start(), calls=%async_computation.2 | async-start | bytes 2605056 | tf_op jit(solution)/shard_map/psum | solution.py:130
  1147.6 55.6 %copy-start.20 = (f32[2,24]{1,0:T(2,128)S(1)}, f32[2,24]{1,0:T(2,128)}, u32[]{:S(2)}) copy-start(f32[2,24]{1,0:T(2,128)} %param.19) | copy-start | bytes 580
  1149.9 53.8 %copy-start.17 = (f32[2,24,2240]{2,1,0:T(8,128)S(1)}, f32[2,24,2240]{2,1,0:T(8,128)}, u32[]{:S(2)}) copy-start(f32[2,24,2240]{2,1,0:T(8,128)} %param.18) | copy-start | bytes 1290244
  1149.9 53.8 %copy-start.18 = (f32[2,24,2240]{2,1,0:T(8,128)S(1)}, f32[2,24,2240]{2,1,0:T(8,128)}, u32[]{:S(2)}) copy-start(f32[2,24,2240]{2,1,0:T(8,128)} %param.17) | copy-start | bytes 1290244
Sparse Core Ops, SparseCore 0:
  11.2 120.4 all-gather.14
  134.9 78.0 all-gather.16
  227.8 13.1 all-gather.18
  244.0 93.1 all-gather.22
  340.3 78.0 all-gather.20
  441.7 13.1 all-gather.24
  479.2 651.2 all-reduce.10
  1150.1 52.1 all-reduce.8
